TPU v7x, 32 devices: a whole 2x2x4 slice. The times are simulated.
32 devices in a mesh: seq: 8 (over z, x), head: 4 (over y, core).
Axes of the slice: x: 2, y: 2, z: 4, core: 2. Of those that a mesh axis runs over, the one named last changes fastest.
Arguments:
- tokens: bfloat16 [2048, 2560], P(('seq', 'head')), may hold values from -6 to 6
- w_xz: bfloat16 [2560, 2, 5120], P(None, None, 'head'), may hold values from -0.125 to 0.125
- w_bc: bfloat16 [2560, 256], replicated, may hold values from -0.125 to 0.125
- w_dt: bfloat16 [2560, 80], P(None, 'head'), may hold values from -0.125 to 0.125
- dt_bias: float32 [80], P('head'), may hold values from -2 to 1
- a_log: float32 [80], P('head'), may hold values from -16 to 0
- conv_x: bfloat16 [4, 5120], P(None, 'head'), may hold values from -3 to 3
- conv_bc: bfloat16 [4, 256], replicated, may hold values from -3 to 3
- norm_gain: float32 [5120], P('head'), may hold values from 0.5 to 1.5
- w_out: bfloat16 [5120, 2560], P('head'), may hold values from -0.078125 to 0.078125
Outputs:
- layer_out: bfloat16 [2048, 2560], P(('seq', 'head'))
All inputs are finite; a program needn't handle non-finite values.
Results may differ from a plain program's by a relative error of at most 0.02.
Values may be sent and summed in bfloat16 or wider, within the bound.
A program may use at most 64 MiB of HBM per device.

v0:
```python
import jax
import jax.numpy as jnp
from jax import lax
from jax.sharding import PartitionSpec as P

SPAN = 256
DI = 5120


def passed_along(value, axis, steps):
    count = lax.axis_size(axis)
    leading, last = (max(0, -steps), min(count, count - steps))
    return lax.ppermute(value, axis, [(source, source + steps) for source in range(leading, last)])


def causal_mix(values, tail_rows, kernel):
    kernel_size = kernel.shape[0]
    row_count = values.shape[0]
    padded = jnp.concatenate([tail_rows, values], axis=0)
    summed = jnp.zeros(values.shape, jnp.float32)
    for offset in range(kernel_size):
        summed = summed + kernel[offset].astype(jnp.float32) * padded[
            offset : offset + row_count
        ].astype(jnp.float32)
    return jax.nn.silu(summed).astype(jnp.bfloat16)


def span_update(carried, inputs):
    value_block, b_block, c_block, step_block, decay_block = inputs
    block_len = value_block.shape[0]
    cumulative = jnp.cumsum(decay_block, axis=0)
    cum_heads = cumulative.T
    differ = cum_heads[:, :, None] - cum_heads[:, None, :]
    causal_mask = (jnp.arange(block_len)[:, None] >= jnp.arange(block_len)[None, :])[None]
    scores = jnp.dot(c_block, b_block.T, preferred_element_type=jnp.float32)
    weights = jnp.where(causal_mask, jnp.exp(jnp.where(causal_mask, differ, 0.0)), 0.0)
    weights = (weights * scores[None] * step_block.T[:, None, :]).astype(jnp.bfloat16)
    start_state = carried.astype(jnp.bfloat16)
    inside = jnp.einsum("hts,shp->thp", weights, value_block, preferred_element_type=jnp.float32)
    carried_out = jnp.exp(cumulative)[:, :, None] * jnp.einsum(
        "tn,hpn->thp", c_block, start_state, preferred_element_type=jnp.float32
    )
    final_decay = cumulative[-1]
    tail_weight = jnp.exp(final_decay[None] - cumulative) * step_block
    scaled = (tail_weight[:, :, None] * value_block.astype(jnp.float32)).astype(jnp.bfloat16)
    new_state = jnp.exp(final_decay)[:, None, None] * carried + jnp.einsum(
        "shp,sn->hpn", scaled, b_block, preferred_element_type=jnp.float32
    )
    return (new_state, inside + carried_out)


def body(tokens, w_xz, w_bc, w_dt, dt_bias, a_log, conv_x, conv_bc, norm_gain, w_out):
    model_width = tokens.shape[1]
    inner_width = w_xz.shape[2]
    head_count = w_dt.shape[1]
    head_width = inner_width // head_count
    state_width = w_bc.shape[1] // 2
    kernel_size = conv_x.shape[0]
    flat_xz = w_xz.reshape(model_width, 2 * inner_width)
    token_piece = lax.all_gather(tokens, "head", axis=0, tiled=True)
    projected = jnp.concatenate(
        [
            jnp.dot(token_piece, flat_xz, preferred_element_type=jnp.float32),
            jnp.dot(token_piece, w_bc, preferred_element_type=jnp.float32),
            jnp.dot(token_piece, w_dt, preferred_element_type=jnp.float32),
        ],
        axis=1,
    )
    row_count = projected.shape[0]
    value_pre = projected[:, :inner_width].astype(jnp.bfloat16)
    gate_pre = projected[:, inner_width : 2 * inner_width].astype(jnp.bfloat16)
    bc_pre = projected[:, 2 * inner_width : 2 * inner_width + 2 * state_width].astype(jnp.bfloat16)
    step_size = jax.nn.softplus(projected[:, 2 * inner_width + 2 * state_width :] + dt_bias[None])
    first_tail = row_count - kernel_size + 1
    value_tail, bc_tail = passed_along((value_pre[first_tail:], bc_pre[first_tail:]), "seq", 1)
    values = causal_mix(value_pre, value_tail, conv_x)
    bc_mixed = causal_mix(bc_pre, bc_tail, conv_bc)
    b_input = bc_mixed[:, :state_width]
    c_input = bc_mixed[:, state_width:]
    log_decay = step_size * (-jnp.exp(a_log))[None]
    blocks = row_count // SPAN
    inputs = (
        values.reshape(blocks, SPAN, head_count, head_width),
        b_input.reshape(blocks, SPAN, state_width),
        c_input.reshape(blocks, SPAN, state_width),
        step_size.reshape(blocks, SPAN, head_count),
        log_decay.reshape(blocks, SPAN, head_count),
    )
    zero_state = jnp.zeros((head_count, head_width, state_width), jnp.float32)
    local_state, outputs = lax.scan(span_update, zero_state, inputs)
    decay_total = jnp.sum(log_decay, axis=0)
    cumulative = jnp.cumsum(log_decay, axis=0)
    totals = lax.all_gather(decay_total[None], "seq", axis=0, tiled=True)
    inclusive = jnp.cumsum(totals, axis=0)
    position = lax.axis_index("seq")
    mine = lax.dynamic_index_in_dim(inclusive - totals, position, 0, keepdims=False)
    shard_piece = lax.all_gather(
        local_state[None].astype(jnp.bfloat16), "seq", axis=0, tiled=True
    ).astype(jnp.float32)
    piece_rows = shard_piece.shape[0]
    sources = jnp.arange(piece_rows, dtype=jnp.int32)
    earlier_mask = (sources < position)[:, None]
    factor = jnp.where(
        earlier_mask, jnp.exp(jnp.where(earlier_mask, mine[None] - inclusive, 0.0)), 0.0
    )
    incoming = zero_state + jnp.einsum(
        "jh,jhpn->hpn", factor, shard_piece, precision=lax.Precision.HIGHEST
    )
    correction = jnp.exp(cumulative)[:, :, None] * jnp.einsum(
        "tn,hpn->thp", c_input, incoming.astype(jnp.bfloat16), preferred_element_type=jnp.float32
    )
    ssm_out = (outputs.reshape(row_count, head_count, head_width) + correction).reshape(
        row_count, inner_width
    )
    gated = ssm_out * jax.nn.silu(gate_pre.astype(jnp.float32))
    square_sum = lax.psum(jnp.sum(gated * gated, axis=1), "head")
    scale = lax.rsqrt(square_sum / DI + 1.0)[:, None]
    normed = (gated * scale * norm_gain[None]).astype(jnp.bfloat16)
    return lax.psum_scatter(
        jnp.dot(normed, w_out, preferred_element_type=jnp.float32).astype(jnp.bfloat16),
        "head",
        scatter_dimension=0,
        tiled=True,
    )


def solution(mesh):
    in_specs = (
        P(("seq", "head"), None),
        P(None, None, "head"),
        P(),
        P(None, "head"),
        P("head"),
        P("head"),
        P(None, "head"),
        P(),
        P("head"),
        P("head", None),
    )
    out_specs = P(("seq", "head"), None)
    return jax.shard_map(body, mesh=mesh, in_specs=in_specs, out_specs=out_specs, check_vma=False)
```

profile of v0, /device:TPU:0, one launch (start us, length us, event | category | flops | bytes accessed | tf_op | source)
XLA Modules:
  0.0 159.0 jit_solution(3188680982576996081)
XLA Ops:
  6.5 0.7 all-gather.5.cloned.1.call-update
  7.3 12.5 %copy.27 = bf16[320,8,2,1280]{3,1,2,0:T(8,128)(2,1)} copy(bf16[320,8,2,1280]{3,2,1,0:T(2,128)(2,1)} %bitcast.60) | data formatting | bytes 26214400
  19.9 9.9 %all-gather.5.cloned.1.call-done = bf16[256,2560]{1,0:T(8,128)(2,1)} async-done(((bf16[64,2560]{1,0:T(8,128)(2,1)}), bf16[256,2560]{1,0:T(8,128)(2,1)}) %all-gather.5.cloned.1.call-update) | async-done | bytes 1310736 | tf_op jit(solution)/shard_map/all_gather | solution.py:60
  29.8 8.8 %convolution_convert_fusion.1 = bf16[256,2560]{1,0:T(8,128)(2,1)S(1)} fusion(bf16[256,2560]{1,0:T(8,128)(2,1)} %all-gather.5.cloned.1.call-done, bf16[2560,2560]{1,0:T(8,128)(2,1)} %bitcast.61), kind=kOutput, calls=%fused_computation.2 | convolution fusion | flops 3356098560 | bytes 15728640 | tf_op jit(solution)/shard_map/dot_general | solution.py:63
  38.6 3.5 %collective-permute-start = (bf16[3,1280]{1,0:T(4,128)(2,1)S(1)}, bf16[3,1280]{1,0:T(4,128)(2,1)S(1)}, u32[]{:S(2)}, u32[]{:S(2)}) collective-permute-start(bf16[3,1280]{1,0:T(4,128)(2,1)S(1)} %slice.98), channel_id=1, source_target_pairs={{0,4},{4,8},{8,12},{12,16},{16,20},{20,24},{24,28},{1,5},{5,9},{9,... | collective-permute-start | bytes 23048 | tf_op jit(solution)/shard_map/ppermute | solution.py:13
  42.2 0.5 convolution_convert_fusion.2
  42.7 3.4 %collective-permute-start.1 = (bf16[3,256]{1,0:T(4,128)(2,1)S(1)}, bf16[3,256]{1,0:T(4,128)(2,1)S(1)}, u32[]{:S(2)}, u32[]{:S(2)}) collective-permute-start(bf16[3,256]{1,0:T(4,128)(2,1)S(1)} %slice.105), channel_id=1, source_target_pairs={{0,4},{4,8},{8,12},{12,16},{16,20},{20,24},{24,28},{1,5},{5,9},{9,... | collective-permute-start | bytes 4616 | tf_op jit(solution)/shard_map/ppermute | solution.py:13
  46.1 0.5 broadcast_multiply_fusion
  46.6 0.6 reduce-window.12
  47.2 0.2 slice_reduce_fusion
  47.6 0.2 slice_reduce_fusion.1
  47.7 0.2 exponential_multiply_fusion
  48.0 0.2 multiply_convert_fusion.9
  48.2 0.9 multiply_convert_fusion.6
  49.1 0.2 copy.20
  49.3 1.1 fusion.16
  50.5 0.6 dynamic-slice.4
  51.8 0.2 dynamic-update-slice
  52.0 20.6 %all-reduce = f32[160]{0:T(256)S(1)} all-reduce(f32[160]{0:T(256)S(1)} %dynamic-update-slice), channel_id=2, replica_groups=mesh['seq'=8,'head'=4] {'seq'}, use_global_device_ids=true, to_apply=%add | all-reduce | flops 160 | bytes 1280
  72.8 0.1 select_bitcast_fusion
  72.9 0.1 copy.24
  73.0 0.2 fusion.30
  73.2 1.7 %fusion.9 = f32[256,20,64]{0,2,1:T(8,128)S(1)} fusion(bf16[256,20,64]{0,2,1:T(8,128)(2,1)S(1)} %bitcast.66, f32[20,256]{1,0:T(8,128)S(1)} %get-tuple-element.37, f32[256,256]{1,0:T(8,128)S(1)} %fusion.30, f32[20,256]{1,0:T(8,128)S(1)} %bitcast.69, pred[256,256]{1,0:T(8,128)(4,1)S(1)} %iota_compare_fusion), kind=kOutput, calls=%fused_computation.14 | convolution fusion | flops 175636480 | bytes 2334720 | tf_op jit(solution)/shard_map/while/body/eval_jaxpr/hts,shp->thp/dot_general | solution.py:39
  74.8 0.3 fusion.11
  75.2 30.2 %all-gather.7.cloned.1.call-done = bf16[160,64,128]{2,1,0:T(8,128)(2,1)} async-done(((bf16[20,64,128]{2,1,0:T(8,128)(2,1)}), bf16[160,64,128]{2,1,0:T(8,128)(2,1)}) %all-gather.7.cloned.1.call-update) | async-done | bytes 2621456 | tf_op jit(solution)/shard_map/all_gather | solution.py:97
  105.4 4.9 %fusion.1 = f32[20,1,64,128]{3,1,2,0:T(1,128)S(1)} fusion(f32[8,20,1,1]{0,2,3,1:T(1,128)S(1)} %copy.24, bf16[8,20,64,128]{3,2,1,0:T(8,128)(2,1)} %bitcast.63), kind=kOutput, calls=%fused_computation.4 | convolution fusion | flops 15728640 | bytes 3277440 | tf_op jit(solution)/shard_map/jh,jhpn->hpn/dot_general | solution.py:106
  110.3 1.4 fusion.10
  111.7 1.7 %copy.23 = f32[256,1280]{1,0:T(8,128)S(1)} copy(f32[256,1280]{0,1:T(8,128)} %bitcast.62) | data formatting | bytes 2621440 | tf_op jit(solution)/shard_map/reshape | solution.py:112
  113.4 1.6 multiply_reduce_fusion
  115.0 5.7 %psum.7 = f32[256]{0:T(256)S(1)} all-reduce(f32[256]{0:T(256)S(1)} %multiply_reduce_fusion), channel_id=1, replica_groups=mesh['seq'=8,'head'=4] {'head'}, use_global_device_ids=true, to_apply=%region_5.6 | all-reduce | flops 256 | bytes 2048 | tf_op jit(solution)/shard_map/psum | solution.py:116
  120.7 6.3 %convolution_convert_fusion = bf16[256,2560]{1,0:T(8,128)(2,1)} fusion(bf16[1280,2560]{1,0:T(8,128)(2,1)} %param.19, f32[1280]{0:T(1024)S(1)} %copy-done.7, f32[256]{0:T(256)S(1)} %add_rsqrt_fusion, f32[256,1280]{1,0:T(8,128)S(1)} %copy.23, bf16[256,2560]{1,0:T(8,128)(2,1)} %copy-done.1), kind=kOutput, calls=%fused_computation.1 | convolution fusion | flops 1681326080 | bytes 9836544 | tf_op jit(solution)/shard_map/dot_general | solution.py:120
  127.0 25.5 %reduce-scatter.2.cloned.1.call-done = bf16[64,2560]{1,0:T(8,128)(2,1)} async-done(((bf16[256,2560]{1,0:T(8,128)(2,1)}), bf16[64,2560]{1,0:T(8,128)(2,1)}) %reduce-scatter.2.cloned.1.call-update) | async-done | bytes 327696 | tf_op jit(solution)/shard_map/reduce_scatter | solution.py:119
  (50 shorter events, 0.7 us)
Async XLA Ops:
  6.5 35.6 %copy-start = (bf16[2560,256]{1,0:T(8,128)(2,1)S(1)}, bf16[2560,256]{1,0:T(8,128)(2,1)}, u32[]{:S(2)}) copy-start(bf16[2560,256]{1,0:T(8,128)(2,1)} %param.12) | copy-start | bytes 3932164
  6.5 23.3 %all-gather.5.cloned.1.call-start = ((), (), s32[]{:S(2)}) async-start(), calls=%async_computation.1 | async-start | bytes 1638400 | tf_op jit(solution)/shard_map/all_gather | solution.py:60
  7.3 98.2 %all-gather.7.cloned.1.call-start = ((), (), s32[]{:S(2)}) async-start(), calls=%async_computation.3 | async-start | bytes 2949120 | tf_op jit(solution)/shard_map/all_gather | solution.py:97
  7.3 12.5 %copy-start.4 = (bf16[4,1280]{1,0:T(4,128)(2,1)S(1)}, bf16[4,1280]{1,0:T(4,128)(2,1)}, u32[]{:S(2)}) copy-start(bf16[4,1280]{1,0:T(4,128)(2,1)} %param.16) | copy-start | bytes 30724
  7.3 12.5 %copy-start.8 = (f32[20]{0:T(128)S(1)}, f32[20]{0:T(128)}, u32[]{:S(2)}) copy-start(f32[20]{0:T(128)} %param.15) | copy-start | bytes 244
  7.3 12.6 %copy-start.5 = (bf16[4,256]{1,0:T(4,128)(2,1)S(1)}, bf16[4,256]{1,0:T(4,128)(2,1)}, u32[]{:S(2)}) copy-start(bf16[4,256]{1,0:T(4,128)(2,1)} %param.17) | copy-start | bytes 6148
  29.8 12.3 %copy-start.2 = (bf16[256,2560]{1,0:T(8,128)(2,1)S(1)}, bf16[256,2560]{1,0:T(8,128)(2,1)}, u32[]{:S(2)}) copy-start(bf16[256,2560]{1,0:T(8,128)(2,1)} %all-gather.5.cloned.1.call-done) | copy-start | bytes 3932164
  38.6 9.3 %copy-start.1 = (bf16[256,2560]{1,0:T(8,128)(2,1)}, bf16[256,2560]{1,0:T(8,128)(2,1)S(1)}, u32[]{:S(2)}) copy-start(bf16[256,2560]{1,0:T(8,128)(2,1)S(1)} %convolution_convert_fusion.1) | copy-start | bytes 3932164
  38.6 7.5 %copy-start.3 = (bf16[2560,20]{0,1:T(8,128)(2,1)S(1)}, bf16[2560,20]{0,1:T(8,128)(2,1)}, u32[]{:S(2)}) copy-start(bf16[2560,20]{0,1:T(8,128)(2,1)} %param.13) | copy-start | bytes 307204
  38.6 7.5 %copy-start.6 = (f32[20]{0:T(128)S(1)}, f32[20]{0:T(128)}, u32[]{:S(2)}) copy-start(f32[20]{0:T(128)} %param.14) | copy-start | bytes 244
  38.6 9.6 %collective-permute-start = (bf16[3,1280]{1,0:T(4,128)(2,1)S(1)}, bf16[3,1280]{1,0:T(4,128)(2,1)S(1)}, u32[]{:S(2)}, u32[]{:S(2)}) collective-permute-start(bf16[3,1280]{1,0:T(4,128)(2,1)S(1)} %slice.98), channel_id=1, source_target_pairs={{0,4},{4,8},{8,12},{12,16},{16,20},{20,24},{24,28},{1,5},{5,9},{9,... | collective-permute-start | bytes 23048 | tf_op jit(solution)/shard_map/ppermute | solution.py:13
  42.7 5.3 %collective-permute-start.1 = (bf16[3,256]{1,0:T(4,128)(2,1)S(1)}, bf16[3,256]{1,0:T(4,128)(2,1)S(1)}, u32[]{:S(2)}, u32[]{:S(2)}) collective-permute-start(bf16[3,256]{1,0:T(4,128)(2,1)S(1)} %slice.105), channel_id=1, source_target_pairs={{0,4},{4,8},{8,12},{12,16},{16,20},{20,24},{24,28},{1,5},{5,9},{9,... | collective-permute-start | bytes 4616 | tf_op jit(solution)/shard_map/ppermute | solution.py:13
  49.1 1.4 copy-start.9
  50.4 102.1 %reduce-scatter.2.cloned.1.call-start = ((), (), s32[]{:S(2)}) async-start(), calls=%async_computation.2 | async-start | bytes 1638400 | tf_op jit(solution)/shard_map/reduce_scatter | solution.py:119
  113.4 7.3 %copy-start.7 = (f32[1280]{0:T(1024)S(1)}, f32[1280]{0:T(1024)}, u32[]{:S(2)}) copy-start(f32[1280]{0:T(1024)} %param.18) | copy-start | bytes 15364
Sparse Core Ops, SparseCore 0:
  8.9 20.8 all-gather.4
  50.5 54.8 all-gather.6
  127.1 25.2 reduce-scatter.1
where the time goes:
time: 159 us
  waiting for transfers between devices  66.4 us (42%)
  blocking collectives  26.3 us (17%)
  matrix products  25.6 us (16%)
  local copies, waits for them, and re-layouts  15.9 us (10%)
  between operations  14.1 us (9%)
  starting transfers between devices  6.98 us (4%)
  other arithmetic  3.75 us (2%)
    all_gather x1, waiting for transfers between devices, body(): lax.all_gather(local_state[None].astype(jnp.bfloat16), 'seq', axis=0, til...  30.2 us
    reduce_scatter x1, waiting for transfers between devices, body(): lax.psum_scatter(jnp.dot(normed, w_out, preferred_element_type=jnp.float3...  25.5 us
    unnamed x1, blocking collectives  20.6 us
    unnamed x26, local copies, waits for them, and re-layouts  13.4 us
    all_gather x1, waiting for transfers between devices, body(): token_piece = lax.all_gather(tokens, 'head', axis=0, tiled=True)  9.92 us
    dot_general x1, matrix products, body(): jnp.dot(token_piece, flat_xz, preferred_element_type=jnp.float32)  8.76 us
    ppermute x2, starting transfers between devices, passed_along(): lax.ppermute(value, axis, [(source, source + steps) for source in range(l...  6.89 us
    dot_general x1, matrix products, body(): jnp.dot(normed, w_out, preferred_element_type=jnp.float32)  6.32 us
  transfers between devices with their start and end apart: 5, of which 3 were waited for; matrix products, arithmetic and copies ran while one was open for 12% of the time, Pallas kernels for 0%

commit v1 on v0

v1 whole, which is shorter than its diff:
```python
import functools

import jax
import jax.numpy as jnp
from jax import lax
from jax.experimental import pallas as pl
from jax.experimental.pallas import tpu as pltpu
from jax.sharding import PartitionSpec as P

F32 = jnp.float32
BF16 = jnp.bfloat16
MESH = pl.DeviceIdType.MESH
HALO = 16
NK = 5
NJ = 5
NP = 5
NT = (((1,), (1,)), ((), ()))
TN = (((0,), (0,)), ((), ()))


def dot(a, b, dims=(((1,), (0,)), ((), ())), precision=None):
    return lax.dot_general(a, b, dims, precision=precision, preferred_element_type=F32)


def silu(v):
    return v / (1.0 + jnp.exp(-v))


def softplus(v):
    return jnp.maximum(v, 0.0) + jnp.log1p(jnp.exp(-jnp.abs(v)))


def kernel(
    n_seq, n_head,
    tokens, w_hbm, wbc, wdt, dtb, alog, cvx, cvbc, gain, wo_hbm,
    out,
    wbuf, wobuf, xbuf, xint, emat, acc, bcbuf, cstep, ccum, rstep, rcum, vals, masked,
    st, stb, ra, dmine, dpart, pin, pout, tpart, sin, yacc, gbuf, sqs, sqr, sqs2, sqr2, sqown,
    pbuf, s1, r1, s2, r2, own,
    wsem, wosem, halo_s, halo_r, core_s, core_r, y_s, y_r, f_s, f_r,
    d_s, d_r, a_s, a_r, c_s, c_r, t_s, t_r, q_s, q_r, q2_s, q2_r, e_s, e_r, g_s, g_r,
):
    s = lax.axis_index("seq")
    h = lax.axis_index("head")
    R, K = tokens.shape
    N = w_hbm.shape[2]
    HL = wdt.shape[0]
    hw = N // HL
    ny = n_head // 2
    y, c = h // 2, h % 2
    other = y * 2 + (1 - c)
    z, x = s // 2, s % 2
    nz = n_seq // 2
    rows = R * n_head
    full = rows + HALO
    kc = K // NK
    D = wo_hbm.shape[1]
    jc = D // NJ
    last = n_head - 1

    def remote(src, dst, ss, rs, ts, th):
        return pltpu.make_async_remote_copy(
            src_ref=src, dst_ref=dst, send_sem=ss, recv_sem=rs, device_id=(ts, th), device_id_type=MESH)

    wcp = [pltpu.make_async_copy(w_hbm.at[pl.ds(k * kc, kc)], wbuf.at[k], wsem.at[k]) for k in range(NK)]
    for cp in wcp:
        cp.start()
    wocp = [
        pltpu.make_async_copy(wo_hbm.at[:, pl.ds(j * jc, jc)], wobuf.at[j], wosem.at[j]) for j in range(NJ)
    ]
    for cp in wocp:
        cp.start()

    bar = pltpu.get_barrier_semaphore()

    def hello(ts, th):
        pl.semaphore_signal(bar, inc=1, device_id=(ts, th), device_id_type=MESH)

    for d in range(1, n_head):
        hello(s, (h + d) % n_head)
    mate = s + 1 - 2 * x
    hello(mate, h)

    @pl.when(z > 0)
    def _():
        hello(s - 2, h)

    @pl.when(z < nz - 1)
    def _():
        hello(s + 2, h)

    @pl.when(s > 0)
    def _():
        hello(s - 1, last)

    @pl.when(jnp.logical_and(h == last, s < n_seq - 1))
    def _():
        for d in range(n_head):
            hello(s + 1, d)

    wait = n_head + jnp.where(z > 0, 1, 0) + jnp.where(z < nz - 1, 1, 0) + jnp.where(s > 0, 1, 0)
    wait = wait + jnp.where(jnp.logical_and(h == last, s < n_seq - 1), n_head, 0)

    def block(hh):
        return pl.ds(pl.multiple_of(HALO + hh * R, 16), R)

    xbuf[block(h), :] = tokens[...]

    @pl.when(s == 0)
    def _():
        xbuf[0:HALO, :] = jnp.zeros((HALO, K), BF16)

    er = lax.broadcasted_iota(jnp.int32, (256, 512), 0)
    ec = lax.broadcasted_iota(jnp.int32, (256, 512), 1)
    emat[0] = jnp.where(ec == 2 * er, 1.0, 0.0).astype(BF16)
    emat[1] = jnp.where(ec == 2 * er + 1, 1.0, 0.0).astype(BF16)
    pl.semaphore_wait(bar, wait)

    @pl.when(jnp.logical_and(h == last, s < n_seq - 1))
    def _():
        for d in range(n_head):
            remote(tokens.at[pl.ds(R - HALO, HALO)], xbuf.at[pl.ds(0, HALO)], halo_s.at[d], halo_r,
                   s + 1, d).start()

    def core_copy(k):
        return remote(tokens.at[:, pl.ds(k * kc, kc)], xbuf.at[block(h), pl.ds(k * kc, kc)],
                      core_s.at[k], core_r.at[k], s, other)

    def y_copy(k, d):
        return remote(tokens.at[:, pl.ds(k * kc, kc)], xbuf.at[block(h), pl.ds(k * kc, kc)],
                      y_s.at[d, k], y_r.at[d, k], s, ((y + d) % ny) * 2 + c)

    def f_copy(k, d):
        part = xbuf.at[block(((y + ny - d) % ny) * 2 + c), pl.ds(k * kc, kc)]
        return remote(part, part, f_s.at[d, k], f_r.at[d, k], s, other)

    for k in range(NK):
        for d in range(1, ny):
            y_copy(k, d).start()
        core_copy(k).start()

    def forward(k):
        for d in range(1, ny):
            y_copy(k, d).wait_recv()
            f_copy(k, d).start()

    forward(0)

    @pl.when(s > 0)
    def _():
        remote(tokens.at[pl.ds(R - HALO, HALO)], xbuf.at[pl.ds(0, HALO)], halo_s.at[0], halo_r,
               s, h).wait_recv()

    for k in range(NK):
        if k + 1 < NK:
            forward(k + 1)
        core_copy(k).wait_recv()
        for d in range(1, ny):
            f_copy(k, d).wait_recv()
        for b in range(kc // 256):
            piece = xbuf[:, k * kc + b * 256:k * kc + (b + 1) * 256]
            xint[0:full, b * 512:(b + 1) * 512] = dot(piece, emat[0]).astype(BF16)
            xint[full:2 * full, b * 512:(b + 1) * 512] = dot(piece, emat[1]).astype(BF16)
        wcp[k].wait()

        def columns(n, _):
            cols = pl.ds(pl.multiple_of(n * 256, 128), 256)
            w = wbuf[k, :, :, cols].reshape(2 * kc, 256)
            got = dot(xint[...], w)
            if k == 0:
                acc[:, cols] = got
            else:
                acc[:, cols] += got
            return 0

        if N % 256 == 0:
            lax.fori_loop(0, N // 256, columns, 0)
        else:
            got = dot(xint[...], wbuf[k].reshape(2 * kc, N))
            acc[...] = got if k == 0 else acc[...] + got

    xs = xbuf[HALO:full, :]
    eye = (lax.broadcasted_iota(jnp.int32, (HL, HL), 0) == lax.broadcasted_iota(jnp.int32, (HL, HL), 1))
    brow = dtb[...]
    rrow = -jnp.exp(alog[...])
    bcol = jnp.sum(jnp.where(eye, brow, 0.0), axis=1, keepdims=True)
    rcol = jnp.sum(jnp.where(eye, rrow, 0.0), axis=1, keepdims=True)
    step_c = softplus(dot(xs, wdt[...], NT) + brow)
    step_r = softplus(dot(wdt[...], xs, NT) + bcol)
    ti = lax.broadcasted_iota(jnp.int32, (rows, rows), 0)
    si = lax.broadcasted_iota(jnp.int32, (rows, rows), 1)
    lower = jnp.where(ti >= si, 1.0, 0.0)
    cum_c = dot(lower, step_c * rrow, precision=lax.Precision.HIGHEST)
    cum_r = dot(step_r * rcol, lower, NT, precision=lax.Precision.HIGHEST)
    cstep[...] = step_c
    ccum[...] = cum_c
    rstep[...] = step_r
    rcum[...] = cum_r
    end_r = cum_r[:, rows - 1:rows]
    dmine[...] = jnp.broadcast_to(end_r, (HL, 128))
    dcopy = remote(dmine, dpart, d_s, d_r, mate, h)
    dcopy.start()

    bcbuf[...] = dot(xbuf[...], wbc[...])
    pre = bcbuf[...].astype(BF16).astype(F32)
    taps = cvbc[...].astype(F32)
    mixed = jnp.zeros((rows, pre.shape[1]), F32)
    n_tap = taps.shape[0]
    for k in range(n_tap):
        shift = n_tap - 1 - k
        moved = pltpu.roll(pre, shift, 0) if shift else pre
        mixed = mixed + taps[k:k + 1, :] * moved[HALO:full]
    mixed = silu(mixed).astype(BF16)
    sw = mixed.shape[1] // 2
    b_in = mixed[:, :sw]
    c_in = mixed[:, sw:]
    masked[...] = jnp.where(ti >= si, dot(c_in, b_in, NT), 0.0)

    lane = lax.broadcasted_iota(jnp.int32, (rows, 128), 1)
    hlane = lax.broadcasted_iota(jnp.int32, (rows, HL), 1)
    per = 128 // hw

    def pick(arr, i):
        return jnp.sum(jnp.where(hlane == i, arr, 0.0), axis=1, keepdims=True)

    def spread(arr, p):
        got = pick(arr, p * per)
        for i in range(1, per):
            got = jnp.where(lane >= i * hw, pick(arr, p * per + i), got)
        return jnp.broadcast_to(got, (rows, 128))

    def own_state(p, _):
        cols = pl.ds(pl.multiple_of(p * 128, 128), 128)
        pre = acc[0:full, cols].astype(BF16).astype(F32)
        taps = cvx[:, cols].astype(F32)
        mixed = jnp.zeros((rows, 128), F32)
        for k in range(n_tap):
            shift = n_tap - 1 - k
            moved = pltpu.roll(pre, shift, 0) if shift else pre
            mixed = mixed + taps[k:k + 1, :] * moved[HALO:full]
        v = silu(mixed).astype(BF16)
        vals[:, cols] = v
        cum = ccum[...]
        tail = jnp.exp(cum[rows - 1:rows, :] - cum) * cstep[...]
        scaled = (spread(tail, p) * v.astype(F32)).astype(BF16)
        got = dot(scaled, b_in, TN)
        st[cols, :] = got
        stb[cols, :] = got.astype(BF16)
        return 0

    n_pair = N // 128
    lax.fori_loop(0, n_pair, own_state, 0)

    half = N // 2
    pr = half // NP
    ph = pr // hw

    def piece(ref, which, i):
        return ref.at[pl.ds(pl.multiple_of(which * half + i * pr, 16), pr)]

    def a_copy(i):
        return remote(piece(stb, 1 - x, i), ra.at[i], a_s.at[i], a_r.at[i], mate, h)

    def c_copy(i):
        return remote(pout.at[i], pin.at[i], c_s.at[i], c_r.at[i], s + 2, h)

    def t_copy(i):
        return remote(tpart.at[i], piece(sin, x, i), t_s.at[i], t_r.at[i], mate, h)

    for i in range(NP):
        a_copy(i).start()

    def inside(p, _):
        cols = pl.ds(pl.multiple_of(p * 128, 128), 128)
        v = vals[:, cols]
        cum = ccum[...]
        total = None
        for i in range(per):
            head = p * per + i
            away = pick(cum, head) - rcum[pl.ds(head, 1), :]
            w = jnp.exp(jnp.minimum(away, 0.0)) * masked[...] * rstep[pl.ds(head, 1), :]
            got = dot(w.astype(BF16), v)
            total = got if i == 0 else jnp.where(lane >= i * hw, got, total)
        yacc[:, cols] = total
        return 0

    early = (n_pair * (z + 1)) // nz
    lax.fori_loop(0, early, inside, 0)

    dcopy.wait_recv()

    @pl.when(z == 0)
    def _():
        for i in range(NP):
            pin[i] = jnp.zeros((pr, sw), BF16)

    for i in range(NP):
        a_copy(i).wait_recv()

        @pl.when(z > 0)
        def _():
            c_copy(i).wait_recv()

        for g in range(ph):
            head = x * (half // hw) + i * ph + g
            part = pl.ds(g * hw, hw)
            mine = jnp.exp(dmine[pl.ds(head, 1), :])
            theirs = jnp.exp(dpart[pl.ds(head, 1), :])
            d0 = jnp.where(x == 0, mine, theirs)
            d1 = jnp.where(x == 0, theirs, mine)
            mst = st[pl.ds(pl.multiple_of(head * hw, hw), hw), :]
            tst = ra[i, part, :].astype(F32)
            first = jnp.where(x == 0, mst, tst)
            second = jnp.where(x == 0, tst, mst)
            start = pin[i, part, :].astype(F32)
            after = d0 * start + first
            pout[i, part, :] = (d1 * after + second).astype(BF16)
            tpart[i, part, :] = jnp.where(x == 0, after, start).astype(BF16)
            sin[pl.ds(pl.multiple_of(head * hw, hw), hw), :] = jnp.where(x == 0, start, after).astype(BF16)

        @pl.when(z < nz - 1)
        def _():
            c_copy(i).start()

        t_copy(i).start()

    lax.fori_loop(early, n_pair, inside, 0)

    for i in range(NP):
        t_copy(i).wait_recv()

    def gate_part(p, total):
        cols = pl.ds(pl.multiple_of(p * 128, 128), 128)
        from_state = dot(c_in, sin[cols, :], NT)
        ssm = yacc[:, cols] + spread(jnp.exp(ccum[...]), p) * from_state
        gate = acc[full + HALO:2 * full, cols].astype(BF16).astype(F32)
        gated = ssm * silu(gate)
        gbuf[:, cols] = (gated * gain[:, cols]).astype(BF16)
        return total + gated * gated

    squares = lax.fori_loop(0, n_pair, gate_part, jnp.zeros((rows, 128), F32))
    pbuf[:, 0:128] = jnp.broadcast_to(jnp.sum(squares, axis=1, keepdims=True), (rows, 128))

    def rows_of(yy, cc):
        return pl.ds(pl.multiple_of((yy * 2 + cc) * R, 16), R)

    for yy in range(ny):
        sqs[yy] = pbuf[rows_of(yy, 1 - c), 0:128]
        sqown[yy] = pbuf[rows_of(yy, c), 0:128]
    q_copy = remote(sqs, sqr, q_s, q_r, s, other)
    q_copy.start()

    def q2_copy(d):
        return remote(sqs2.at[d], sqr2.at[d], q2_s.at[d], q2_r.at[d], s, ((y + d) % ny) * 2 + c)

    def e_copy(j):
        return remote(s1.at[j], r1.at[j], e_s.at[j], e_r.at[j], s, other)

    def g_copy(j, d):
        return remote(s2.at[j, d], r2.at[j, d], g_s.at[j, d], g_r.at[j, d], s, ((y + d) % ny) * 2 + c)

    def product(j):
        wocp[j].wait()
        pbuf[...] = dot(gbuf[...], wobuf[j])
        for yy in range(ny):
            s1[j, yy] = pbuf[rows_of(yy, 1 - c), :].astype(BF16)
        e_copy(j).start()
        for yy in range(ny):
            own[j, yy] = pbuf[rows_of(yy, c), :]

    def pass_on(j):
        e_copy(j).wait_recv()
        for d in range(1, ny):
            yy = (y + d) % ny
            s2[j, d] = (own[j, yy] + r1[j, yy].astype(F32)).astype(BF16)
            g_copy(j, d).start()

    product(0)
    q_copy.wait_recv()
    for d in range(1, ny):
        yy = (y + d) % ny
        sqs2[d] = sqown[yy] + sqr[yy]
        q2_copy(d).start()
    for j in range(1, NJ):
        product(j)
        pass_on(j - 1)
    pass_on(NJ - 1)

    square = sqown[y] + sqr[y]
    for d in range(1, ny):
        q2_copy(d).wait_recv()
        square = square + sqr2[d]
    scale = lax.rsqrt(square[:, 0:1] / (N * n_head) + 1.0)
    for j in range(NJ):
        total = own[j, y] + r1[j, y].astype(F32)
        for d in range(1, ny):
            g_copy(j, d).wait_recv()
            total = total + r2[j, d].astype(F32)
        out[:, j * jc:(j + 1) * jc] = (total * scale).astype(BF16)

    @pl.when(jnp.logical_and(h == last, s < n_seq - 1))
    def _():
        for d in range(n_head):
            remote(tokens.at[pl.ds(R - HALO, HALO)], xbuf.at[pl.ds(0, HALO)], halo_s.at[d], halo_r,
                   s + 1, d).wait_send()

    for k in range(NK):
        core_copy(k).wait_send()
        for d in range(1, ny):
            y_copy(k, d).wait_send()
            f_copy(k, d).wait_send()
    dcopy.wait_send()
    for i in range(NP):
        a_copy(i).wait_send()
        t_copy(i).wait_send()

    @pl.when(z < nz - 1)
    def _():
        for i in range(NP):
            c_copy(i).wait_send()

    q_copy.wait_send()
    for d in range(1, ny):
        q2_copy(d).wait_send()
    for j in range(NJ):
        e_copy(j).wait_send()
        for d in range(1, ny):
            g_copy(j, d).wait_send()


def body(n_seq, n_head, tokens, w_xz, w_bc, w_dt, dt_bias, a_log, conv_x, conv_bc, norm_gain, w_out):
    R, K = tokens.shape
    N = w_xz.shape[2]
    HL = w_dt.shape[1]
    D = w_out.shape[1]
    bc = w_bc.shape[1]
    sw = bc // 2
    rows = R * n_head
    full = rows + HALO
    ny = n_head // 2
    kc, jc, pr = K // NK, D // NJ, N // 2 // NP
    V = pltpu.VMEM
    dma = pltpu.SemaphoreType.DMA
    vm = pl.BlockSpec(memory_space=pltpu.VMEM)
    anyspace = pl.BlockSpec(memory_space=pl.ANY)
    scratch = [
        V((NK, kc, 2, N), BF16), V((NJ, N, jc), BF16), V((full, K), BF16), V((2 * full, 2 * kc), BF16),
        V((2, 256, 512), BF16), V((2 * full, N), F32), V((full, bc), F32),
        V((rows, HL), F32), V((rows, HL), F32), V((HL, rows), F32), V((HL, rows), F32),
        V((rows, N), BF16), V((rows, rows), F32),
        V((N, sw), F32), V((N, sw), BF16), V((NP, pr, sw), BF16), V((HL, 128), F32), V((HL, 128), F32),
        V((NP, pr, sw), BF16), V((NP, pr, sw), BF16), V((NP, pr, sw), BF16), V((N, sw), BF16),
        V((rows, N), F32), V((rows, N), BF16),
        V((ny, R, 128), F32), V((ny, R, 128), F32), V((ny, R, 128), F32), V((ny, R, 128), F32),
        V((ny, R, 128), F32),
        V((rows, jc), F32), V((NJ, ny, R, jc), BF16), V((NJ, ny, R, jc), BF16),
        V((NJ, ny, R, jc), BF16), V((NJ, ny, R, jc), BF16), V((NJ, ny, R, jc), F32),
        dma((NK,)), dma((NJ,)), dma((n_head,)), dma, dma((NK,)), dma((NK,)),
        dma((ny, NK)), dma((ny, NK)), dma((ny, NK)), dma((ny, NK)),
        dma, dma, dma((NP,)), dma((NP,)), dma((NP,)), dma((NP,)), dma((NP,)), dma((NP,)),
        dma, dma, dma((ny,)), dma((ny,)), dma((NJ,)), dma((NJ,)), dma((NJ, ny)), dma((NJ, ny)),
    ]
    return pl.pallas_call(
        functools.partial(kernel, n_seq, n_head),
        out_shape=jax.ShapeDtypeStruct((R, D), BF16),
        in_specs=[vm, anyspace, vm, vm, vm, vm, vm, vm, vm, anyspace],
        out_specs=vm,
        scratch_shapes=scratch,
        compiler_params=pltpu.CompilerParams(
            collective_id=0, has_side_effects=True, vmem_limit_bytes=62 * 2**20),
    )(tokens, w_xz, w_bc, w_dt.T, dt_bias[None], a_log[None], conv_x, conv_bc, norm_gain[None], w_out)


def solution(mesh):
    in_specs = (
        P(("seq", "head"), None),
        P(None, None, "head"),
        P(),
        P(None, "head"),
        P("head"),
        P("head"),
        P(None, "head"),
        P(),
        P("head"),
        P("head", None),
    )
    out_specs = P(("seq", "head"), None)
    run = functools.partial(body, mesh.shape["seq"], mesh.shape["head"])
    return jax.shard_map(run, mesh=mesh, in_specs=in_specs, out_specs=out_specs, check_vma=False)
```

time: 159 us -> 64.7 us (0.41)
  the two profiles are of different devices: /device:TPU:0 before, /device:TPU:31 now
where the time goes in v1:
time: 64.7 us; the launch traced here: 64.5 us
  Pallas kernels  61.5 us (95%)
  local copies, waits for them, and re-layouts  3.01 us (5%)
    pallas_call x1, Pallas kernels, body(): pl.pallas_call(functools.partial(kernel, n_seq, n_head), out_shape=jax.Sh...  61.5 us
    unnamed x1, local copies, waits for them, and re-layouts  1.72 us

profile of v1, /device:TPU:31, one launch (start us, length us, event | category | flops | bytes accessed | tf_op | source)
XLA Modules:
  0.0 64.5 jit_solution(14003045935749764504)
XLA Ops:
  0.0 1.3 %broadcast_in_dim.11.gain = f32[1,1280]{1,0:T(1,128)} reshape(f32[1280]{0:T(1024)} %param.18) | data formatting | bytes 10240 | tf_op jit(solution)/shard_map/broadcast_in_dim | solution.py:471
  1.3 61.5 %shard_map.100 = bf16[64,2560]{1,0:T(8,128)(2,1)} custom-call(bf16[64,2560]{1,0:T(8,128)(2,1)} %tokens.1, bf16[2560,2,1280]{2,1,0:T(2,128)(2,1)} %w_hbm.1, bf16[2560,256]{1,0:T(8,128)(2,1)} %wbc.1, bf16[20,2560]{1,0:T(8,128)(2,1)} %bitcast.3, f32[1,20]{1,0:T(1,128)} %bitcast.4, f32[1,20]{1,0:T(1,128)} %bitcast.5, bf16[4,1280]{1,0:T(4,128)(2,1)} %cvx.1, ...), custom_call_target="tpu_custom_call" | custom-call | tf_op jit(solution)/shard_map/pallas_call | solution.py:463
  62.8 1.7 %copy.12 = bf16[64,2560]{1,0:T(8,128)(2,1)} copy(bf16[64,2560]{1,0:T(8,128)(2,1)} %shard_map.100) | data formatting | bytes 655360

commit v2 on v1

--- a/solution.py
+++ b/solution.py
@@ -10,7 +10,7 @@
 F32 = jnp.float32
 BF16 = jnp.bfloat16
 MESH = pl.DeviceIdType.MESH
-HALO = 16
+HALO = 8
 NK = 5
 NJ = 5
 NP = 5
@@ -32,12 +32,12 @@
 
 def kernel(
     n_seq, n_head,
-    tokens, w_hbm, wbc, wdt, dtb, alog, cvx, cvbc, gain, wo_hbm,
+    tokens, w_hbm, wbc_hbm, wdt, dtb, alog, cvx, cvbc, gain1, wo_hbm,
     out,
-    wbuf, wobuf, xbuf, xint, emat, acc, bcbuf, cstep, ccum, rstep, rcum, vals, masked,
+    wbuf, wobuf, wbc, gain, tailb, edge, esg, xbuf, xint, emat, acc, bcbuf, ccum, rstep, rcum, vals, masked,
     st, stb, ra, dmine, dpart, pin, pout, tpart, sin, yacc, gbuf, sqs, sqr, sqs2, sqr2, sqown,
     pbuf, s1, r1, s2, r2, own,
-    wsem, wosem, halo_s, halo_r, core_s, core_r, y_s, y_r, f_s, f_r,
+    wsem, wosem, bcsem, halo_s, halo_r, core_s, core_r, y_s, y_r, f_s, f_r,
     d_s, d_r, a_s, a_r, c_s, c_r, t_s, t_r, q_s, q_r, q2_s, q2_r, e_s, e_r, g_s, g_r,
 ):
     s = lax.axis_index("seq")
@@ -57,6 +57,7 @@
     D = wo_hbm.shape[1]
     jc = D // NJ
     last = n_head - 1
+    wide = N // 2 if N % 256 == 0 else N
 
     def remote(src, dst, ss, rs, ts, th):
         return pltpu.make_async_remote_copy(
@@ -65,6 +66,8 @@
     wcp = [pltpu.make_async_copy(w_hbm.at[pl.ds(k * kc, kc)], wbuf.at[k], wsem.at[k]) for k in range(NK)]
     for cp in wcp:
         cp.start()
+    bccp = pltpu.make_async_copy(wbc_hbm, wbc, bcsem)
+    bccp.start()
     wocp = [
         pltpu.make_async_copy(wo_hbm.at[:, pl.ds(j * jc, jc)], wobuf.at[j], wosem.at[j]) for j in range(NJ)
     ]
@@ -102,7 +105,7 @@
     wait = wait + jnp.where(jnp.logical_and(h == last, s < n_seq - 1), n_head, 0)
 
     def block(hh):
-        return pl.ds(pl.multiple_of(HALO + hh * R, 16), R)
+        return pl.ds(pl.multiple_of(HALO + hh * R, 8), R)
 
     xbuf[block(h), :] = tokens[...]
 
@@ -110,10 +113,10 @@
     def _():
         xbuf[0:HALO, :] = jnp.zeros((HALO, K), BF16)
 
+    gain[...] = gain1[...].reshape(1, N)
     er = lax.broadcasted_iota(jnp.int32, (256, 512), 0)
     ec = lax.broadcasted_iota(jnp.int32, (256, 512), 1)
-    emat[0] = jnp.where(ec == 2 * er, 1.0, 0.0).astype(BF16)
-    emat[1] = jnp.where(ec == 2 * er + 1, 1.0, 0.0).astype(BF16)
+    emat[...] = jnp.where(ec == 2 * er, 1.0, 0.0).astype(BF16)
     pl.semaphore_wait(bar, wait)
 
     @pl.when(jnp.logical_and(h == last, s < n_seq - 1))
@@ -159,13 +162,16 @@
             f_copy(k, d).wait_recv()
         for b in range(kc // 256):
             piece = xbuf[:, k * kc + b * 256:k * kc + (b + 1) * 256]
-            xint[0:full, b * 512:(b + 1) * 512] = dot(piece, emat[0]).astype(BF16)
-            xint[full:2 * full, b * 512:(b + 1) * 512] = dot(piece, emat[1]).astype(BF16)
+            even = dot(piece, emat[...])
+            xint[0:full, b * 512:(b + 1) * 512] = even.astype(BF16)
+            for q in range(4):
+                odd = pltpu.roll(even[:, q * 128:(q + 1) * 128], 1, 1)
+                xint[full:2 * full, b * 512 + q * 128:b * 512 + (q + 1) * 128] = odd.astype(BF16)
         wcp[k].wait()
 
         def columns(n, _):
-            cols = pl.ds(pl.multiple_of(n * 256, 128), 256)
-            w = wbuf[k, :, :, cols].reshape(2 * kc, 256)
+            cols = pl.ds(pl.multiple_of(n * wide, 128), wide)
+            w = wbuf[k, :, :, cols].reshape(2 * kc, wide)
             got = dot(xint[...], w)
             if k == 0:
                 acc[:, cols] = got
@@ -173,11 +179,7 @@
                 acc[:, cols] += got
             return 0
 
-        if N % 256 == 0:
-            lax.fori_loop(0, N // 256, columns, 0)
-        else:
-            got = dot(xint[...], wbuf[k].reshape(2 * kc, N))
-            acc[...] = got if k == 0 else acc[...] + got
+        lax.fori_loop(0, N // wide, columns, 0)
 
     xs = xbuf[HALO:full, :]
     eye = (lax.broadcasted_iota(jnp.int32, (HL, HL), 0) == lax.broadcasted_iota(jnp.int32, (HL, HL), 1))
@@ -192,15 +194,17 @@
     lower = jnp.where(ti >= si, 1.0, 0.0)
     cum_c = dot(lower, step_c * rrow, precision=lax.Precision.HIGHEST)
     cum_r = dot(step_r * rcol, lower, NT, precision=lax.Precision.HIGHEST)
-    cstep[...] = step_c
     ccum[...] = cum_c
     rstep[...] = step_r
     rcum[...] = cum_r
+    tailb[...] = jnp.exp(cum_c[rows - 1:rows, :] - cum_c) * step_c
+    edge[...] = jnp.exp(cum_c)
     end_r = cum_r[:, rows - 1:rows]
     dmine[...] = jnp.broadcast_to(end_r, (HL, 128))
     dcopy = remote(dmine, dpart, d_s, d_r, mate, h)
     dcopy.start()
 
+    bccp.wait()
     bcbuf[...] = dot(xbuf[...], wbc[...])
     pre = bcbuf[...].astype(BF16).astype(F32)
     taps = cvbc[...].astype(F32)
@@ -229,7 +233,10 @@
             got = jnp.where(lane >= i * hw, pick(arr, p * per + i), got)
         return jnp.broadcast_to(got, (rows, 128))
 
-    def own_state(p, _):
+    n_pair = N // 128
+
+    def own_state(i, _):
+        p = (i + (1 - x) * (n_pair // 2)) % n_pair
         cols = pl.ds(pl.multiple_of(p * 128, 128), 128)
         pre = acc[0:full, cols].astype(BF16).astype(F32)
         taps = cvx[:, cols].astype(F32)
@@ -240,16 +247,13 @@
             mixed = mixed + taps[k:k + 1, :] * moved[HALO:full]
         v = silu(mixed).astype(BF16)
         vals[:, cols] = v
-        cum = ccum[...]
-        tail = jnp.exp(cum[rows - 1:rows, :] - cum) * cstep[...]
-        scaled = (spread(tail, p) * v.astype(F32)).astype(BF16)
+        scaled = (spread(tailb[...], p) * v.astype(F32)).astype(BF16)
         got = dot(scaled, b_in, TN)
         st[cols, :] = got
         stb[cols, :] = got.astype(BF16)
         return 0
 
-    n_pair = N // 128
-    lax.fori_loop(0, n_pair, own_state, 0)
+    lax.fori_loop(0, (n_pair + 1) // 2, own_state, 0)
 
     half = N // 2
     pr = half // NP
@@ -269,6 +273,8 @@
 
     for i in range(NP):
         a_copy(i).start()
+
+    lax.fori_loop((n_pair + 1) // 2, n_pair, own_state, 0)
 
     def inside(p, _):
         cols = pl.ds(pl.multiple_of(p * 128, 128), 128)
@@ -281,7 +287,9 @@
             w = jnp.exp(jnp.minimum(away, 0.0)) * masked[...] * rstep[pl.ds(head, 1), :]
             got = dot(w.astype(BF16), v)
             total = got if i == 0 else jnp.where(lane >= i * hw, got, total)
-        yacc[:, cols] = total
+        gate = silu(acc[full + HALO:2 * full, cols].astype(BF16).astype(F32))
+        yacc[:, cols] = total * gate
+        esg[:, cols] = spread(edge[...], p) * gate
         return 0
 
     early = (n_pair * (z + 1)) // nz
@@ -332,9 +340,7 @@
     def gate_part(p, total):
         cols = pl.ds(pl.multiple_of(p * 128, 128), 128)
         from_state = dot(c_in, sin[cols, :], NT)
-        ssm = yacc[:, cols] + spread(jnp.exp(ccum[...]), p) * from_state
-        gate = acc[full + HALO:2 * full, cols].astype(BF16).astype(F32)
-        gated = ssm * silu(gate)
+        gated = yacc[:, cols] + esg[:, cols] * from_state
         gbuf[:, cols] = (gated * gain[:, cols]).astype(BF16)
         return total + gated * gated
 
@@ -444,9 +450,10 @@
     vm = pl.BlockSpec(memory_space=pltpu.VMEM)
     anyspace = pl.BlockSpec(memory_space=pl.ANY)
     scratch = [
-        V((NK, kc, 2, N), BF16), V((NJ, N, jc), BF16), V((full, K), BF16), V((2 * full, 2 * kc), BF16),
-        V((2, 256, 512), BF16), V((2 * full, N), F32), V((full, bc), F32),
-        V((rows, HL), F32), V((rows, HL), F32), V((HL, rows), F32), V((HL, rows), F32),
+        V((NK, kc, 2, N), BF16), V((NJ, N, jc), BF16), V((K, bc), BF16), V((1, N), F32),
+        V((rows, HL), F32), V((rows, HL), F32), V((rows, N), F32), V((full, K), BF16), V((2 * full, 2 * kc), BF16),
+        V((256, 512), BF16), V((2 * full, N), F32), V((full, bc), F32),
+        V((rows, HL), F32), V((HL, rows), F32), V((HL, rows), F32),
         V((rows, N), BF16), V((rows, rows), F32),
         V((N, sw), F32), V((N, sw), BF16), V((NP, pr, sw), BF16), V((HL, 128), F32), V((HL, 128), F32),
         V((NP, pr, sw), BF16), V((NP, pr, sw), BF16), V((NP, pr, sw), BF16), V((N, sw), BF16),
@@ -455,7 +462,7 @@
         V((ny, R, 128), F32),
         V((rows, jc), F32), V((NJ, ny, R, jc), BF16), V((NJ, ny, R, jc), BF16),
         V((NJ, ny, R, jc), BF16), V((NJ, ny, R, jc), BF16), V((NJ, ny, R, jc), F32),
-        dma((NK,)), dma((NJ,)), dma((n_head,)), dma, dma((NK,)), dma((NK,)),
+        dma((NK,)), dma((NJ,)), dma, dma((n_head,)), dma, dma((NK,)), dma((NK,)),
         dma((ny, NK)), dma((ny, NK)), dma((ny, NK)), dma((ny, NK)),
         dma, dma, dma((NP,)), dma((NP,)), dma((NP,)), dma((NP,)), dma((NP,)), dma((NP,)),
         dma, dma, dma((ny,)), dma((ny,)), dma((NJ,)), dma((NJ,)), dma((NJ, ny)), dma((NJ, ny)),
@@ -463,12 +470,12 @@
     return pl.pallas_call(
         functools.partial(kernel, n_seq, n_head),
         out_shape=jax.ShapeDtypeStruct((R, D), BF16),
-        in_specs=[vm, anyspace, vm, vm, vm, vm, vm, vm, vm, anyspace],
+        in_specs=[vm, anyspace, anyspace, vm, vm, vm, vm, vm, vm, anyspace],
         out_specs=vm,
         scratch_shapes=scratch,
         compiler_params=pltpu.CompilerParams(
             collective_id=0, has_side_effects=True, vmem_limit_bytes=62 * 2**20),
-    )(tokens, w_xz, w_bc, w_dt.T, dt_bias[None], a_log[None], conv_x, conv_bc, norm_gain[None], w_out)
+    )(tokens, w_xz, w_bc, w_dt.T, dt_bias[None], a_log[None], conv_x, conv_bc, norm_gain, w_out)
 
 
 def solution(mesh):

time: 64.7 us -> 58 us (0.90)
  Pallas kernels: 61.5 us -> 56.1 us
  local copies, waits for them, and re-layouts: 3.01 us -> 1.72 us
    pallas_call x1, Pallas kernels: 61.5 us -> 56.1 us  [body(): pl.pallas_call(functools.partial(kernel, n_seq, n_head), out_shape=jax.Sh...]
    broadcast_in_dim x1 -> x0, local copies, waits for them, and re-layouts: 1.29 us -> none  [body(): norm_gain[None]]
where the time goes in v2:
time: 58 us; the launch traced here: 57.9 us
  Pallas kernels  56.1 us (97%)
  local copies, waits for them, and re-layouts  1.72 us (3%)
    pallas_call x1, Pallas kernels, body(): pl.pallas_call(functools.partial(kernel, n_seq, n_head), out_shape=jax.Sh...  56.1 us
    unnamed x1, local copies, waits for them, and re-layouts  1.72 us

profile of v2, /device:TPU:31, one launch (start us, length us, event | category | flops | bytes accessed | tf_op | source)
XLA Modules:
  0.0 57.9 jit_solution(4843898041632137197)
XLA Ops:
  0.0 56.1 %shard_map.100 = bf16[64,2560]{1,0:T(8,128)(2,1)} custom-call(bf16[64,2560]{1,0:T(8,128)(2,1)} %tokens.1, bf16[2560,2,1280]{2,1,0:T(2,128)(2,1)} %w_hbm.1, bf16[2560,256]{1,0:T(8,128)(2,1)} %wbc_hbm.1, bf16[20,2560]{1,0:T(8,128)(2,1)} %bitcast.3, f32[1,20]{1,0:T(1,128)} %bitcast.4, f32[1,20]{1,0:T(1,128)} %bitcast.5, bf16[4,1280]{1,0:T(4,128)(2,1)} %cvx.1, ...), custom_call_target="tpu_custom_call" | custom-call | tf_op jit(solution)/shard_map/pallas_call | solution.py:470
  56.1 1.7 %copy.12 = bf16[64,2560]{1,0:T(8,128)(2,1)} copy(bf16[64,2560]{1,0:T(8,128)(2,1)} %shard_map.100) | data formatting | bytes 655360

commit v3 on v2

--- a/solution.py
+++ b/solution.py
@@ -34,7 +34,7 @@
     n_seq, n_head,
     tokens, w_hbm, wbc_hbm, wdt, dtb, alog, cvx, cvbc, gain1, wo_hbm,
     out,
-    wbuf, wobuf, wbc, gain, tailb, edge, esg, xbuf, xint, emat, acc, bcbuf, ccum, rstep, rcum, vals, masked,
+    wbuf, wobuf, wbc, gain, tailb, edge, esg, xbuf, xint, xodd, gacc, emat, acc, bcbuf, ccum, rstep, rcum, vals, masked,
     st, stb, ra, dmine, dpart, pin, pout, tpart, sin, yacc, gbuf, sqs, sqr, sqs2, sqr2, sqown,
     pbuf, s1, r1, s2, r2, own,
     wsem, wosem, bcsem, halo_s, halo_r, core_s, core_r, y_s, y_r, f_s, f_r,
@@ -163,10 +163,10 @@
         for b in range(kc // 256):
             piece = xbuf[:, k * kc + b * 256:k * kc + (b + 1) * 256]
             even = dot(piece, emat[...])
-            xint[0:full, b * 512:(b + 1) * 512] = even.astype(BF16)
+            xint[:, b * 512:(b + 1) * 512] = even.astype(BF16)
             for q in range(4):
                 odd = pltpu.roll(even[:, q * 128:(q + 1) * 128], 1, 1)
-                xint[full:2 * full, b * 512 + q * 128:b * 512 + (q + 1) * 128] = odd.astype(BF16)
+                xodd[k, :, b * 512 + q * 128:b * 512 + (q + 1) * 128] = odd[HALO:full].astype(BF16)
         wcp[k].wait()
 
         def columns(n, _):
@@ -287,12 +287,24 @@
             w = jnp.exp(jnp.minimum(away, 0.0)) * masked[...] * rstep[pl.ds(head, 1), :]
             got = dot(w.astype(BF16), v)
             total = got if i == 0 else jnp.where(lane >= i * hw, got, total)
-        gate = silu(acc[full + HALO:2 * full, cols].astype(BF16).astype(F32))
+        gate = silu(gacc[:, cols].astype(BF16).astype(F32))
         yacc[:, cols] = total * gate
         esg[:, cols] = spread(edge[...], p) * gate
         return 0
 
+    gw = 256 if N % 256 == 0 else 128
+
+    def gates(n, _):
+        cols = pl.ds(pl.multiple_of(n * gw, 128), gw)
+        got = dot(xodd[0], wbuf[0, :, :, cols].reshape(2 * kc, gw))
+        for k in range(1, NK):
+            got = got + dot(xodd[k], wbuf[k, :, :, cols].reshape(2 * kc, gw))
+        gacc[:, cols] = got
+        return 0
+
     early = (n_pair * (z + 1)) // nz
+    early_g = (early * 128 + gw - 1) // gw
+    lax.fori_loop(0, early_g, gates, 0)
     lax.fori_loop(0, early, inside, 0)
 
     dcopy.wait_recv()
@@ -332,6 +344,7 @@
 
         t_copy(i).start()
 
+    lax.fori_loop(early_g, N // gw, gates, 0)
     lax.fori_loop(early, n_pair, inside, 0)
 
     for i in range(NP):
@@ -451,8 +464,9 @@
     anyspace = pl.BlockSpec(memory_space=pl.ANY)
     scratch = [
         V((NK, kc, 2, N), BF16), V((NJ, N, jc), BF16), V((K, bc), BF16), V((1, N), F32),
-        V((rows, HL), F32), V((rows, HL), F32), V((rows, N), F32), V((full, K), BF16), V((2 * full, 2 * kc), BF16),
-        V((256, 512), BF16), V((2 * full, N), F32), V((full, bc), F32),
+        V((rows, HL), F32), V((rows, HL), F32), V((rows, N), F32), V((full, K), BF16), V((full, 2 * kc), BF16),
+        V((NK, rows, 2 * kc), BF16), V((rows, N), F32),
+        V((256, 512), BF16), V((full, N), F32), V((full, bc), F32),
         V((rows, HL), F32), V((HL, rows), F32), V((HL, rows), F32),
         V((rows, N), BF16), V((rows, rows), F32),
         V((N, sw), F32), V((N, sw), BF16), V((NP, pr, sw), BF16), V((HL, 128), F32), V((HL, 128), F32),

time: 58 us -> 54.7 us (0.943)
  Pallas kernels: 56.1 us -> 52.3 us
    pallas_call x1, Pallas kernels: 56.1 us -> 52.3 us  [body(): pl.pallas_call(functools.partial(kernel, n_seq, n_head), out_shape=jax.Sh...]
where the time goes in v3:
time: 54.7 us; the launch traced here: 54 us
  Pallas kernels  52.3 us (96%)
  local copies, waits for them, and re-layouts  1.72 us (3%)
    pallas_call x1, Pallas kernels, body(): pl.pallas_call(functools.partial(kernel, n_seq, n_head), out_shape=jax.Sh...  52.3 us
    unnamed x1, local copies, waits for them, and re-layouts  1.72 us

profile of v3, /device:TPU:31, one launch (start us, length us, event | category | flops | bytes accessed | tf_op | source)
XLA Modules:
  0.0 54.0 jit_solution(6868711330618799266)
XLA Ops:
  0.0 52.3 %shard_map.100 = bf16[64,2560]{1,0:T(8,128)(2,1)} custom-call(bf16[64,2560]{1,0:T(8,128)(2,1)} %tokens.1, bf16[2560,2,1280]{2,1,0:T(2,128)(2,1)} %w_hbm.1, bf16[2560,256]{1,0:T(8,128)(2,1)} %wbc_hbm.1, bf16[20,2560]{1,0:T(8,128)(2,1)} %bitcast.3, f32[1,20]{1,0:T(1,128)} %bitcast.4, f32[1,20]{1,0:T(1,128)} %bitcast.5, bf16[4,1280]{1,0:T(4,128)(2,1)} %cvx.1, ...), custom_call_target="tpu_custom_call" | custom-call | tf_op jit(solution)/shard_map/pallas_call | solution.py:484
  52.3 1.7 %copy.12 = bf16[64,2560]{1,0:T(8,128)(2,1)} copy(bf16[64,2560]{1,0:T(8,128)(2,1)} %shard_map.100) | data formatting | bytes 655360
